TPU v7x, 128 devices: a whole 4x4x4 slice. The times are simulated.
128 devices in a mesh: grp: 2 (over x_lo), dp: 64 (over y, x_hi, z, core).
Axes of the slice: x: 4 (x_hi: 2, x_lo: 2; x = x_hi * 2 + x_lo), y: 4, z: 4, core: 2. Of those that a mesh axis runs over, the one named last changes fastest.
Arguments:
- teacher_in: bfloat16 [32768, 1664], P('dp'), may hold values from -6 to 6
- teacher_gain: float32 [1664], replicated, may hold values from 0.5 to 1.5
- teacher_up: bfloat16 [1664, 4096], P('dp', 'grp'), may hold values from -0.15625 to 0.15625
- teacher_down: bfloat16 [1664, 4096], P('dp', 'grp'), may hold values from -0.09375 to 0.09375
- student_in: bfloat16 [32768, 768], P('dp'), may hold values from -6 to 6
- student_gain: float32 [768], replicated, may hold values from 0.5 to 1.5
- student_up: bfloat16 [768, 1536], P(None, ('grp', 'dp')), may hold values from -0.21875 to 0.21875
- student_down: bfloat16 [1536, 768], P(('grp', 'dp')), may hold values from -0.15625 to 0.15625
- student_head: bfloat16 [768, 1664], P(None, ('grp', 'dp')), may hold values from -0.21875 to 0.21875
- student_proj: bfloat16 [768, 512], P(None, ('grp', 'dp')), may hold values from -1 to 1
- word_table: bfloat16 [49408, 512], P(('grp', 'dp')), may hold values from -6 to 6
- caption_ids: int32 [128, 77], replicated, may hold values from 0 to 49407
- positive: int32 [128], replicated, may hold values from 0 to 127, each once
Outputs:
- loss: float32 [], replicated
- grad_up: float32 [768, 1536], P(None, ('grp', 'dp'))
- grad_down: float32 [1536, 768], P(('grp', 'dp'))
- grad_head: float32 [768, 1664], P(None, ('grp', 'dp'))
- grad_proj: float32 [768, 512], P(None, ('grp', 'dp'))
Inputs may be any that keep to these rules, and one draw needn't show every extreme that they name: Each caption is the positive of exactly one image.
All inputs are finite; a program needn't handle non-finite values.
Results may differ from a plain program's by a relative error of at most 0.0065.
Values may be sent and summed in bfloat16 or wider, within the bound.
A program may use at most 128 MiB of HBM per device.

v0:
```python
import jax
import jax.numpy as jnp
from jax import lax
from jax.sharding import PartitionSpec as P

CAP_LEN = 77
PATCHES = 256
IMG_DEV = 1


def normalize_rows(values, gain):
    center = values - jnp.mean(values, -1, keepdims=True)
    spread = jnp.mean(center * center, -1, keepdims=True)
    return center * lax.rsqrt(spread + 1e-05) * gain


def gelu_tanh(values):
    return jax.nn.gelu(values, approximate=True)


def unit_rows(values):
    return values / jnp.sqrt(jnp.sum(values * values, -1, keepdims=True) + 1e-06)


def local(
    teacher_in,
    teacher_gain,
    teacher_up,
    teacher_down,
    student_in,
    student_gain,
    student_up,
    student_down,
    student_head,
    student_proj,
    word_table,
    caption_ids,
    positive,
):
    contract = (((1,), (1,)), ((), ()))
    grp_index = lax.axis_index("grp")
    dp_index = lax.axis_index("dp")
    n_grp = lax.axis_size("grp")
    n_dp = lax.axis_size("dp")
    devices = n_grp * n_dp
    teacher_width = teacher_in.shape[1]
    rows_teacher = teacher_in.shape[0]
    teacher_normed = normalize_rows(teacher_in.astype(jnp.float32), teacher_gain).astype(
        jnp.bfloat16
    )
    columns = teacher_normed
    hidden = jnp.dot(
        columns,
        lax.all_gather(teacher_up, "dp", axis=0, tiled=True),
        preferred_element_type=jnp.float32,
    )
    teacher_act = gelu_tanh(hidden).astype(jnp.bfloat16)
    partial_value = lax.dot_general(
        teacher_act,
        lax.all_gather(teacher_down, "dp", axis=0, tiled=True),
        contract,
        preferred_element_type=jnp.float32,
    )
    branch = lax.psum_scatter(
        partial_value.astype(jnp.bfloat16), "grp", scatter_dimension=0, tiled=True
    ).astype(jnp.float32)
    own_rows = rows_teacher // n_grp
    target = (
        lax.dynamic_slice_in_dim(teacher_in, grp_index * own_rows, own_rows, 0).astype(jnp.float32)
        + branch
    )
    student_rows = lax.dynamic_slice_in_dim(student_in, grp_index * own_rows, own_rows, 0).astype(
        jnp.float32
    )
    student_width = student_rows.shape[1]
    student_normed = normalize_rows(student_rows, student_gain).astype(jnp.bfloat16)
    gate_out = jnp.dot(
        student_normed,
        lax.all_gather(student_up, ("grp", "dp"), axis=1, tiled=True),
        preferred_element_type=jnp.float32,
    )
    down_whole, head_whole, proj_whole = (
        lax.all_gather(student_down, ("grp", "dp"), axis=0, tiled=True),
        lax.all_gather(student_head, ("grp", "dp"), axis=1, tiled=True),
        lax.all_gather(student_proj, ("grp", "dp"), axis=1, tiled=True),
    )
    student_act = gelu_tanh(gate_out).astype(jnp.bfloat16)
    student_out = student_rows + jnp.dot(
        student_act, down_whole, preferred_element_type=jnp.float32
    )
    student_rounded = student_out.astype(jnp.bfloat16)
    diff = jnp.dot(student_rounded, head_whole, preferred_element_type=jnp.float32) - target
    feature_part = jnp.sum(diff * diff) / teacher_width
    pooled = (jnp.sum(student_out.reshape(IMG_DEV, PATCHES, student_width), 1) / PATCHES).astype(
        jnp.bfloat16
    )
    projected = jnp.dot(pooled, proj_whole, preferred_element_type=jnp.float32)
    proj_norm = jnp.sqrt(jnp.sum(projected * projected, -1, keepdims=True) + 1e-06)
    image_emb = projected / proj_norm
    embed_width = image_emb.shape[1]
    caption_count = caption_ids.shape[0]
    caption_dev = caption_count // devices
    shard_block = grp_index * n_dp + dp_index
    vocab_dev = word_table.shape[0]
    vocab_codes = shard_block * vocab_dev + jnp.arange(vocab_dev, dtype=jnp.int32)
    counts = jnp.sum(
        caption_ids[:, :, None] == vocab_codes[None, None, :], 1, dtype=jnp.float32
    ).astype(jnp.bfloat16)
    partial_words = jnp.dot(counts, word_table, preferred_element_type=jnp.float32) / CAP_LEN
    words = lax.psum(partial_words, ("grp", "dp"))
    caption_all = unit_rows(words)
    caption_own = lax.dynamic_slice_in_dim(caption_all, shard_block * caption_dev, caption_dev, 0)
    gathered = lax.all_gather(image_emb, ("grp", "dp"), axis=0, tiled=True)
    image_all = jnp.transpose(
        gathered.reshape(n_grp, n_dp, IMG_DEV, embed_width), (1, 0, 2, 3)
    ).reshape(-1, embed_width)
    image_first = (dp_index * n_grp + grp_index) * IMG_DEV
    positive_own = lax.dynamic_slice_in_dim(positive, image_first, IMG_DEV, 0)
    scores_own = 100.0 * jnp.dot(image_emb, caption_all.T, precision=lax.Precision.HIGHEST)
    match_own = (
        positive_own[:, None] == jnp.arange(caption_count, dtype=jnp.int32)[None, :]
    ).astype(jnp.float32)
    caption_first = shard_block * caption_dev
    scores_cols = 100.0 * jnp.dot(image_all, caption_own.T, precision=lax.Precision.HIGHEST)
    match_cols = (
        positive[:, None] == (caption_first + jnp.arange(caption_dev, dtype=jnp.int32))[None, :]
    ).astype(jnp.float32)
    contrast_part = jnp.sum(jax.nn.logsumexp(scores_own, 1)) - jnp.sum(match_own * scores_own)
    contrast_part = (
        contrast_part
        + jnp.sum(jax.nn.logsumexp(scores_cols, 0))
        - jnp.sum(match_cols * scores_cols)
    )
    grad_rows = jax.nn.softmax(scores_own, 1) - match_own
    grad_cols = jax.nn.softmax(scores_cols, 0) - match_cols
    grad_far = 100.0 * jnp.dot(grad_cols, caption_own, precision=lax.Precision.HIGHEST)
    grad_far = jnp.transpose(
        grad_far.reshape(n_dp, n_grp, IMG_DEV, embed_width), (1, 0, 2, 3)
    ).reshape(-1, embed_width)
    grad_image = 100.0 * jnp.dot(grad_rows, caption_all, precision=lax.Precision.HIGHEST)
    grad_image = grad_image + lax.psum_scatter(
        grad_far, ("grp", "dp"), scatter_dimension=0, tiled=True
    )
    grad_projected = (
        (grad_image - image_emb * jnp.sum(image_emb * grad_image, -1, keepdims=True)) / proj_norm
    ).astype(jnp.bfloat16)
    proj_part = jnp.dot(pooled.T, grad_projected, preferred_element_type=jnp.float32)
    grad_pooled = lax.dot_general(
        grad_projected, proj_whole, contract, preferred_element_type=jnp.float32
    )
    grad_pred = (2.0 * diff / teacher_width).astype(jnp.bfloat16)
    head_part = jnp.dot(student_rounded.T, grad_pred, preferred_element_type=jnp.float32)
    grad_out = lax.dot_general(grad_pred, head_whole, contract, preferred_element_type=jnp.float32)
    grad_out = (
        (grad_out.reshape(IMG_DEV, PATCHES, student_width) + (grad_pooled / PATCHES)[:, None, :])
        .reshape(-1, student_width)
        .astype(jnp.bfloat16)
    )
    columns = student_act
    grad_down = lax.psum_scatter(
        lax.dot_general(
            columns, grad_out, (((0,), (0,)), ((), ())), preferred_element_type=jnp.float32
        ),
        ("grp", "dp"),
        scatter_dimension=0,
        tiled=True,
    )
    grad_act = lax.dot_general(grad_out, down_whole, contract, preferred_element_type=jnp.float32)
    grad_gate = jax.vjp(gelu_tanh, gate_out)[1](grad_act)[0].astype(jnp.bfloat16)
    up_part = jnp.dot(student_normed.T, grad_gate, preferred_element_type=jnp.float32)
    grad_up, grad_head, grad_proj = (
        lax.psum_scatter(up_part, ("grp", "dp"), scatter_dimension=1, tiled=True),
        lax.psum_scatter(head_part, ("grp", "dp"), scatter_dimension=1, tiled=True),
        lax.psum_scatter(proj_part, ("grp", "dp"), scatter_dimension=1, tiled=True),
    )
    total = lax.psum(feature_part + contrast_part, ("grp", "dp"))
    loss = total / (positive.shape[0] * PATCHES)
    return (loss, grad_up, grad_down, grad_head, grad_proj)


def solution(mesh):
    placed = (
        P("dp", None),
        P(),
        P("dp", "grp"),
        P("dp", "grp"),
        P("dp", None),
        P(),
        P(None, ("grp", "dp")),
        P(("grp", "dp"), None),
        P(None, ("grp", "dp")),
        P(None, ("grp", "dp")),
        P(("grp", "dp"), None),
        P(),
        P(),
    )
    return jax.shard_map(
        local,
        mesh=mesh,
        in_specs=placed,
        out_specs=(
            P(),
            P(None, ("grp", "dp")),
            P(("grp", "dp"), None),
            P(None, ("grp", "dp")),
            P(None, ("grp", "dp")),
        ),
        check_vma=False,
    )
```

profile of v0, /device:TPU:0, one launch (start us, length us, event | category | flops | bytes accessed | tf_op | source)
XLA Modules:
  0.0 1854.7 jit_solution(75165170728293733)
XLA Ops:
  13.5 181.3 %all-gather.6 = bf16[128,4,768]{2,1,0:T(4,128)(2,1)S(1)} all-gather(bf16[1,4,768]{2,1,0:T(4,128)(2,1)} %bitcast.97), channel_id=1, replica_groups=mesh['grp'=2,'dp'=64] {'grp','dp'}, dimensions={0}, use_global_device_ids=true | all-gather | bytes 792576 | tf_op jit(solution)/shard_map/all_gather | solution.py:85
  198.2 156.9 %all-gather.16.cloned.1.call-done = bf16[128,12,768]{2,1,0:T(8,128)(2,1)} async-done(((bf16[1,12,768]{2,1,0:T(8,128)(2,1)}), bf16[128,12,768]{2,1,0:T(8,128)(2,1)}) %all-gather.16.cloned.1.call-update) | async-done | bytes 2359312 | tf_op jit(solution)/shard_map/all_gather | solution.py:83
  355.1 4.9 reshape.194
  360.0 192.2 %all-gather.14.cloned.1.call-done = bf16[128,12,768]{2,1,0:T(8,128)(2,1)} async-done(((bf16[1,12,768]{2,1,0:T(8,128)(2,1)}), bf16[128,12,768]{2,1,0:T(8,128)(2,1)}) %all-gather.14.cloned.1.call-update) | async-done | bytes 2359312 | tf_op jit(solution)/shard_map/all_gather | solution.py:79
  552.2 4.9 reshape.192
  564.1 176.2 %all-gather.7 = f32[128,1,512]{2,1,0:T(1,128)S(1)} all-gather(f32[1,1,512]{2,1,0:T(1,128)S(1)} %bitcast.84), channel_id=2, replica_groups=mesh['grp'=2,'dp'=64] {'grp','dp'}, dimensions={0}, use_global_device_ids=true | all-gather | bytes 264192 | tf_op jit(solution)/shard_map/all_gather | solution.py:113
  756.6 9.1 reshape.200
  765.7 9.1 reshape.198
  774.9 14.7 convolution_convert_fusion
  792.0 99.0 %all-reduce.15.cloned.1.call-done = f32[128,512]{1,0:T(8,128)} async-done(((f32[128,512]{1,0:T(8,128)}), f32[128,512]{1,0:T(8,128)}) %all-reduce.15.cloned.1.call-update) | async-done | bytes 262160
  895.4 191.7 %all-gather.18.cloned.1.call-done = bf16[128,13,768]{2,1,0:T(8,128)(2,1)} async-done(((bf16[1,13,768]{2,1,0:T(8,128)(2,1)}), bf16[128,13,768]{2,1,0:T(8,128)(2,1)}) %all-gather.18.cloned.1.call-update) | async-done | bytes 2555920 | tf_op jit(solution)/shard_map/all_gather | solution.py:84
  1087.1 5.3 reshape.196
  1092.4 25.4 %reduce-scatter.8.cloned.1.call-done = bf16[256,1664]{1,0:T(8,128)(2,1)} async-done(((bf16[512,1664]{1,0:T(8,128)(2,1)}), bf16[256,1664]{1,0:T(8,128)(2,1)}) %reduce-scatter.8.cloned.1.call-update) | async-done | bytes 851984 | tf_op jit(solution)/shard_map/reduce_scatter | solution.py:64
  1124.1 6.1 fusion.45
  1136.8 366.7 %fusion.88 = (f32[768,16]{0,1:T(8,128)S(1)}, f32[16,768]{1,0:T(8,128)S(1)}, f32[768,16]{0,1:T(8,128)S(1)}) fusion(f32[768,1536]{0,1:T(8,128)} %fusion.45, f32[1536,768]{1,0:T(8,128)} %fusion.87, f32[768,1664]{0,1:T(8,128)} %fusion.56), kind=kCustom, calls=%all-reduce-scatter.3 | all-reduce-scatter fusion | flops 4718593 | bytes 14696448
  1516.7 15.9 collective-permute-start.23
  1542.6 4.9 collective-permute-start.17
  1551.4 4.7 collective-permute-start.14
  1558.7 6.5 collective-permute-start.11
  1576.6 4.7 collective-permute-start.5
  1584.0 4.3 collective-permute-start.3
  1627.5 5.5 collective-permute-start.46
  1636.3 5.6 collective-permute-start.43
  1690.2 7.0 collective-permute-start.78
  1707.9 63.5 %psum.15 = f32[]{:T(128)} all-reduce(f32[]{:T(128)S(6)} %add.151), channel_id=1, replica_groups=mesh['grp'=2,'dp'=64] {'grp','dp'}, use_global_device_ids=true, to_apply=%region_17.0 | all-reduce | flops 1 | bytes 8 | tf_op jit(solution)/shard_map/psum | solution.py:176
  1772.1 5.6 concatenate
  1777.7 4.5 collective-permute-start.73
  1787.9 5.1 collective-permute-start.70
  1796.9 24.2 %concatenate.1 = f32[524,768]{1,0:T(8,128)S(1)} concatenate(f32[12,768]{1,0:T(8,128)S(1)} %collective-permute-done.63, f32[16,768]{1,0:T(8,128)S(1)} %collective-permute-done.62, f32[16,768]{1,0:T(8,128)S(1)} %collective-permute-done.61, f32[16,768]{1,0:T(8,128)S(1)} %collective-permute-done.60, f32[16,768]{1,0:T(8,128)S(1)} %collective-permute-done.59, f32[16,768]{1,0:T(8,128)} %copy-done.9, ...), dimensions={0} | concatenate | bytes 3219456
  1825.0 4.4 collective-permute-start.67
  1829.4 4.6 collective-permute-start.66
  1839.5 6.8 concatenate.2
  (349 shorter events, 208.9 us)
Async XLA Ops:
  7.2 188.8 %all-reduce.13.cloned.1.call-start = ((), (), s32[]{:S(2)}) async-start(), calls=%async_computation.2 | async-start | bytes 524288 | tf_op jit(solution)/shard_map/psum | solution.py:110
  10.8 344.3 %all-gather.16.cloned.1.call-start = ((), (), s32[]{:S(2)}) async-start(), calls=%async_computation.4 | async-start | bytes 3170304 | tf_op jit(solution)/shard_map/all_gather | solution.py:83
  11.5 540.6 %all-gather.14.cloned.1.call-start = ((), (), s32[]{:S(2)}) async-start(), calls=%async_computation.3 | async-start | bytes 3170304 | tf_op jit(solution)/shard_map/all_gather | solution.py:79
  12.3 744.3 %all-gather.22.cloned.1.call-start = ((), (), s32[]{:S(2)}) async-start(), calls=%async_computation.7 | async-start | bytes 8519680 | tf_op jit(solution)/shard_map/all_gather | solution.py:60
  12.8 752.9 %all-gather.20.cloned.1.call-start = ((), (), s32[]{:S(2)}) async-start(), calls=%async_computation.6 | async-start | bytes 8519680 | tf_op jit(solution)/shard_map/all_gather | solution.py:54
  13.4 877.6 %all-reduce.15.cloned.1.call-start = ((), (), s32[]{:S(2)}) async-start(), calls=%async_computation.8 | async-start | bytes 524288
  751.8 335.3 %all-gather.18.cloned.1.call-start = ((), (), s32[]{:S(2)}) async-start(), calls=%async_computation.5 | async-start | bytes 3170304 | tf_op jit(solution)/shard_map/all_gather | solution.py:84
  752.6 365.3 %reduce-scatter.8.cloned.1.call-start = ((), (), s32[]{:S(2)}) async-start(), calls=%async_computation.1 | async-start | bytes 2555904 | tf_op jit(solution)/shard_map/reduce_scatter | solution.py:64
  789.5 917.0 %all-reduce.17.cloned.1.call-start = ((), (), s32[]{:S(2)}) async-start(), calls=%async_computation.9 | async-start | bytes 3145728
  1511.4 21.2 %collective-permute-start.27 = (f32[768,16]{0,1:T(8,128)S(1)}, f32[768,16]{0,1:T(8,128)S(1)}, u32[]{:S(2)}, u32[]{:S(2)}) collective-permute-start(f32[768,16]{0,1:T(8,128)S(1)} %get-tuple-element.14), channel_id=1, source_target_pairs={{0,28},{1,29},{2,30},{3,31},{4,32},{5,33},{6,34},{7,35},{8,36},{9,... | collective-permute-start | bytes 147464
  1512.7 21.8 %collective-permute-start.26 = (f32[768,16]{0,1:T(8,128)S(1)}, f32[768,16]{0,1:T(8,128)S(1)}, u32[]{:S(2)}, u32[]{:S(2)}) collective-permute-start(f32[768,16]{0,1:T(8,128)S(1)} %get-tuple-element.14), channel_id=1, source_target_pairs={{0,27},{1,28},{2,29},{3,30},{4,31},{5,32},{6,33},{7,34},{8,35},{9,... | collective-permute-start | bytes 147464
  1514.0 22.9 %collective-permute-start.25 = (f32[768,16]{0,1:T(8,128)S(1)}, f32[768,16]{0,1:T(8,128)S(1)}, u32[]{:S(2)}, u32[]{:S(2)}) collective-permute-start(f32[768,16]{0,1:T(8,128)S(1)} %get-tuple-element.14), channel_id=1, source_target_pairs={{0,26},{1,27},{2,28},{3,29},{4,30},{5,31},{6,32},{7,33},{8,34},{9,... | collective-permute-start | bytes 147464
  1515.3 23.4 %collective-permute-start.24 = (f32[768,16]{0,1:T(8,128)S(1)}, f32[768,16]{0,1:T(8,128)S(1)}, u32[]{:S(2)}, u32[]{:S(2)}) collective-permute-start(f32[768,16]{0,1:T(8,128)S(1)} %get-tuple-element.14), channel_id=1, source_target_pairs={{0,25},{1,26},{2,27},{3,28},{4,29},{5,30},{6,31},{7,32},{8,33},{9,... | collective-permute-start | bytes 147464
  1516.7 24.7 %collective-permute-start.23 = (f32[768,16]{0,1:T(8,128)S(1)}, f32[768,16]{0,1:T(8,128)S(1)}, u32[]{:S(2)}, u32[]{:S(2)}) collective-permute-start(f32[768,16]{0,1:T(8,128)S(1)} %get-tuple-element.14), channel_id=1, source_target_pairs={{0,24},{1,25},{2,26},{3,27},{4,28},{5,29},{6,30},{7,31},{8,32},{9,... | collective-permute-start | bytes 147464
  1558.7 16.4 collective-permute-start.11
  1576.6 17.5 collective-permute-start.5
  1636.3 16.4 collective-permute-start.43
  1679.5 17.8 collective-permute-start.82
  1680.8 18.6 %collective-permute-start.81 = (f32[768,16]{0,1:T(8,128)S(1)}, f32[768,16]{0,1:T(8,128)S(1)}, u32[]{:S(2)}, u32[]{:S(2)}) collective-permute-start(f32[768,16]{0,1:T(8,128)S(1)} %get-tuple-element.16), channel_id=1, source_target_pairs={{0,18},{1,19},{2,20},{3,21},{4,22},{5,23},{6,24},{7,25},{8,26},{9,... | collective-permute-start | bytes 147464
  1682.1 19.9 %collective-permute-start.80 = (f32[768,16]{0,1:T(8,128)S(1)}, f32[768,16]{0,1:T(8,128)S(1)}, u32[]{:S(2)}, u32[]{:S(2)}) collective-permute-start(f32[768,16]{0,1:T(8,128)S(1)} %get-tuple-element.16), channel_id=1, source_target_pairs={{0,17},{1,18},{2,19},{3,20},{4,21},{5,22},{6,23},{7,24},{8,25},{9,... | collective-permute-start | bytes 147464
  1685.3 19.3 %collective-permute-start.79 = (f32[768,16]{0,1:T(8,128)S(1)}, f32[768,16]{0,1:T(8,128)S(1)}, u32[]{:S(2)}, u32[]{:S(2)}) collective-permute-start(f32[768,16]{0,1:T(8,128)S(1)} %get-tuple-element.16), channel_id=1, source_target_pairs={{0,16},{1,17},{2,18},{3,19},{4,20},{5,21},{6,22},{7,23},{8,24},{9,... | collective-permute-start | bytes 147464
  1690.2 87.5 %collective-permute-start.78 = (f32[768,16]{0,1:T(8,128)S(1)}, f32[768,16]{0,1:T(8,128)}, u32[]{:S(2)}, u32[]{:S(2)}) collective-permute-start(f32[768,16]{0,1:T(8,128)S(1)} %get-tuple-element.16), channel_id=1, source_target_pairs={{0,15},{1,16},{2,17},{3,18},{4,19},{5,20},{6,21},{7,22},{8,23},{9,... | collective-permute-start | bytes 147464
  1697.2 85.0 %collective-permute-start.77 = (f32[768,16]{0,1:T(8,128)S(1)}, f32[768,16]{0,1:T(8,128)}, u32[]{:S(2)}, u32[]{:S(2)}) collective-permute-start(f32[768,16]{0,1:T(8,128)S(1)} %get-tuple-element.16), channel_id=1, source_target_pairs={{0,14},{1,15},{2,16},{3,17},{4,18},{5,19},{6,20},{7,21},{8,22},{9,... | collective-permute-start | bytes 147464
  1699.4 84.6 %collective-permute-start.76 = (f32[768,16]{0,1:T(8,128)S(1)}, f32[768,16]{0,1:T(8,128)}, u32[]{:S(2)}, u32[]{:S(2)}) collective-permute-start(f32[768,16]{0,1:T(8,128)S(1)} %get-tuple-element.16), channel_id=1, source_target_pairs={{0,13},{1,14},{2,15},{3,16},{4,17},{5,18},{6,19},{7,20},{8,21},{9,... | collective-permute-start | bytes 147464
  1702.0 85.9 %collective-permute-start.75 = (f32[768,16]{0,1:T(8,128)S(1)}, f32[768,16]{0,1:T(8,128)}, u32[]{:S(2)}, u32[]{:S(2)}) collective-permute-start(f32[768,16]{0,1:T(8,128)S(1)} %get-tuple-element.16), channel_id=1, source_target_pairs={{0,12},{1,13},{2,14},{3,15},{4,16},{5,17},{6,18},{7,19},{8,20},{9,... | collective-permute-start | bytes 147464
  1704.6 88.4 %collective-permute-start.74 = (f32[768,16]{0,1:T(8,128)S(1)}, f32[768,16]{0,1:T(8,128)}, u32[]{:S(2)}, u32[]{:S(2)}) collective-permute-start(f32[768,16]{0,1:T(8,128)S(1)} %get-tuple-element.16), channel_id=1, source_target_pairs={{0,11},{1,12},{2,13},{3,14},{4,15},{5,16},{6,17},{7,18},{8,19},{9,... | collective-permute-start | bytes 147464
  1777.7 43.4 %collective-permute-start.73 = (f32[768,16]{0,1:T(8,128)S(1)}, f32[768,16]{0,1:T(8,128)S(1)}, u32[]{:S(2)}, u32[]{:S(2)}) collective-permute-start(f32[768,16]{0,1:T(8,128)S(1)} %get-tuple-element.16), channel_id=1, source_target_pairs={{0,10},{1,11},{2,12},{3,13},{4,14},{5,15},{6,16},{7,17},{8,18},{9,... | collective-permute-start | bytes 147464
  1782.2 42.8 %collective-permute-start.72 = (f32[768,16]{0,1:T(8,128)S(1)}, f32[768,16]{0,1:T(8,128)S(1)}, u32[]{:S(2)}, u32[]{:S(2)}) collective-permute-start(f32[768,16]{0,1:T(8,128)S(1)} %get-tuple-element.16), channel_id=1, source_target_pairs={{0,9},{1,10},{2,11},{3,12},{4,13},{5,14},{6,15},{7,16},{8,17},{9,1... | collective-permute-start | bytes 147464
  1784.0 45.4 %collective-permute-start.71 = (f32[768,16]{0,1:T(8,128)S(1)}, f32[768,16]{0,1:T(8,128)S(1)}, u32[]{:S(2)}, u32[]{:S(2)}) collective-permute-start(f32[768,16]{0,1:T(8,128)S(1)} %get-tuple-element.16), channel_id=1, source_target_pairs={{0,8},{1,9},{2,10},{3,11},{4,12},{5,13},{6,14},{7,15},{8,16},{9,17... | collective-permute-start | bytes 147464
  1787.9 46.1 %collective-permute-start.70 = (f32[768,16]{0,1:T(8,128)S(1)}, f32[768,16]{0,1:T(8,128)S(1)}, u32[]{:S(2)}, u32[]{:S(2)}) collective-permute-start(f32[768,16]{0,1:T(8,128)S(1)} %get-tuple-element.16), channel_id=1, source_target_pairs={{0,7},{1,8},{2,9},{3,10},{4,11},{5,12},{6,13},{7,14},{8,15},{9,16}... | collective-permute-start | bytes 147464
  1793.0 44.2 %collective-permute-start.69 = (f32[768,16]{0,1:T(8,128)S(1)}, f32[768,16]{0,1:T(8,128)S(1)}, u32[]{:S(2)}, u32[]{:S(2)}) collective-permute-start(f32[768,16]{0,1:T(8,128)S(1)} %get-tuple-element.16), channel_id=1, source_target_pairs={{0,6},{1,7},{2,8},{3,9},{4,10},{5,11},{6,12},{7,13},{8,14},{9,15},... | collective-permute-start | bytes 147464
  1821.1 18.1 collective-permute-start.68
  (120 other events, 3441.8 us)
Sparse Core Ops, SparseCore 0:
  12.7 146.2 all-reduce.12
  160.7 194.2 all-gather.15
  356.8 195.3 all-gather.13
  555.3 79.8 all-gather.21
  638.2 80.1 all-gather.19
  751.9 139.0 all-reduce.14
  892.7 194.2 all-gather.17
  1089.4 28.3 reduce-scatter.7
  1122.6 152.6 all-reduce.16
where the time goes:
time: 1870 us; the launch traced here: 1850 us
  blocking collectives  788 us (42%)
  waiting for transfers between devices  669 us (36%)
  starting transfers between devices  234 us (13%)
  local copies, waits for them, and re-layouts  80.9 us (4%)
  matrix products  41.4 us (2%)
  between operations  24.5 us (1%)
    unnamed x1, blocking collectives  367 us
    unnamed x90, starting transfers between devices  233 us
    all_gather x1, waiting for transfers between devices, local(): lax.all_gather(student_up, ('grp', 'dp'), axis=1, tiled=True)  192 us
    all_gather x1, waiting for transfers between devices, local(): lax.all_gather(student_head, ('grp', 'dp'), axis=1, tiled=True)  192 us
    all_gather x1, blocking collectives, local(): lax.all_gather(student_proj, ('grp', 'dp'), axis=1, tiled=True)  181 us
    all_gather x1, blocking collectives, local(): gathered = lax.all_gather(image_emb, ('grp', 'dp'), axis=0, tiled=True)  176 us
    all_gather x1, waiting for transfers between devices, local(): lax.all_gather(student_down, ('grp', 'dp'), axis=0, tiled=True)  157 us
    unnamed x99, waiting for transfers between devices  103 us
  transfers between devices with their start and end apart: 97, of which 6 were waited for; matrix products, arithmetic and copies ran while one was open for 27% of the time, Pallas kernels for 0%

commit v1 on v0

v1 whole, which is shorter than its diff:
```python
import jax
import jax.numpy as jnp
from jax import lax
from jax.experimental import pallas as pl
from jax.experimental.pallas import tpu as pltpu
from jax.sharding import PartitionSpec as P

CAP_LEN = 77
PATCHES = 256
BLK = 16
MESH = pl.DeviceIdType.MESH
ANY = pl.BlockSpec(memory_space=pl.ANY)
VM = pl.BlockSpec(memory_space=pltpu.VMEM)


def coords():
    grp = lax.axis_index("grp")
    dp = lax.axis_index("dp")
    x_hi = (dp // 8) % 2
    return {
        "x": 2 * x_hi + grp,
        "y": dp // 16,
        "z": (dp // 2) % 4,
        "core": dp % 2,
    }


def device(at):
    return (at["x"] % 2, at["y"] * 16 + (at["x"] // 2) * 8 + at["z"] * 2 + at["core"])


def shifted(me, axis, step):
    if axis == "core":
        return {**me, "core": 1 - me["core"]}
    return {**me, axis: (me[axis] + step) % 4}


def enter(me, axes=("x", "y", "z"), steps=(1, 2, 3)):
    barrier = pltpu.get_barrier_semaphore()
    peers = [shifted(me, "core", 1)]
    for axis in axes:
        for step in steps:
            peers.append(shifted(me, axis, step))
    for peer in peers:
        pl.semaphore_signal(barrier, inc=1, device_id=device(peer), device_id_type=MESH)
    pl.semaphore_wait(barrier, len(peers))


class Copies:
    def __init__(self, send, recv):
        self.send, self.recv, self.count, self.open = send, recv, 0, []

    def start(self, src, dst, peer):
        copy = pltpu.make_async_remote_copy(
            src_ref=src,
            dst_ref=dst,
            send_sem=self.send.at[self.count],
            recv_sem=self.recv.at[self.count],
            device_id=device(peer),
            device_id_type=MESH,
        )
        self.count += 1
        copy.start()
        self.open.append(copy)
        return copy

    def finish(self):
        for copy in self.open:
            copy.wait_send()


def pick(ref, at, tail=()):
    x = at.get("x")
    whole = slice(None)
    index = (
        whole if x is None else x % 2,
        at.get("y", whole),
        whole if x is None else x // 2,
        at.get("z", whole),
    )
    if "core" in at:
        index += (at["core"],)
    return ref.at[index + tail]


def half(ref, side):
    size = ref.shape[0] // 2
    return ref.at[pl.ds(side * size, size)]


def weight_gather(ins, outs, send, recv, local_sem):
    me = coords()
    enter(me)
    copies = Copies(send, recv)
    sibling = shifted(me, "core", 1)
    locals_ = []
    for i in range(6):
        own = pick_out(outs[i], me, i < 2)
        copy = pltpu.make_async_copy(ins[i], own, local_sem.at[i])
        copy.start()
        locals_.append(copy)

    def push(pushes, view):
        pushes.append(copies.start(view, view, sibling))

    def chain(i, order):
        teacher = i < 2
        out = outs[i]
        pushes = []
        pushes.append(copies.start(ins[i], pick_out(out, me, teacher), sibling))
        held = dict(me)
        first = True
        for axis in order:
            if axis == "xh":
                other = shifted(me, "x", 2)
                copy = copies.start(ins[i], pick_out(out, me, True), other)
                yield
                copy.wait_recv()
                push(pushes, pick_out(out, other, True))
                locals_[i].wait()
                first = False
                held.pop("x")
                continue
            up, down, far = (shifted(me, axis, s) for s in (1, 3, 2))
            block = pick_out(out, held, teacher)
            source = ins[i] if first else block
            right = copies.start(source, block, up)
            left = copies.start(source, block, down)
            yield
            right.wait_recv()
            from_down = pick_out(out, {**held, axis: down[axis]}, teacher)
            right2 = copies.start(half(from_down, 0), half(from_down, 0), up)
            push(pushes, from_down)
            left.wait_recv()
            from_up = pick_out(out, {**held, axis: up[axis]}, teacher)
            left2 = copies.start(half(from_up, 1), half(from_up, 1), down)
            push(pushes, from_up)
            if first:
                locals_[i].wait()
                first = False
            yield
            right2.wait_recv()
            left2.wait_recv()
            push(pushes, pick_out(out, {**held, axis: far[axis]}, teacher))
            held.pop(axis)
        yield
        for copy in pushes:
            copy.wait_recv()

    chains = [
        chain(2, ("y", "z", "x")),
        chain(3, ("z", "y", "x")),
        chain(4, ("y", "z", "x")),
        chain(5, ("z", "y", "x")),
        chain(0, ("xh", "y", "z")),
        chain(1, ("xh", "z", "y")),
    ]
    while chains:
        alive = []
        for one in chains:
            try:
                next(one)
                alive.append(one)
            except StopIteration:
                pass
        chains = alive
    copies.finish()


def pick_out(ref, at, teacher):
    if not teacher:
        return pick(ref, at)
    whole = slice(None)
    x = at.get("x")
    return ref.at[
        (
            at.get("y", whole),
            whole if x is None else x // 2,
            at.get("z", whole),
            at["core"],
        )
    ]


def weight_kernel(*refs):
    ins, outs = refs[:6], refs[6:12]
    weight_gather(ins, outs, *refs[12:])


def gather_weights(parts):
    outs = []
    for i, part in enumerate(parts):
        lead = (4, 2, 4, 2) if i < 2 else (2, 4, 2, 4, 2)
        outs.append(jax.ShapeDtypeStruct(lead + part.shape, part.dtype))
    return pl.pallas_call(
        weight_kernel,
        out_shape=outs,
        in_specs=[ANY] * 6,
        out_specs=[ANY] * 6,
        scratch_shapes=[
            pltpu.SemaphoreType.DMA((122,)),
            pltpu.SemaphoreType.DMA((122,)),
            pltpu.SemaphoreType.DMA((6,)),
        ],
        compiler_params=pltpu.CompilerParams(collective_id=1, has_side_effects=True),
        name="gather_weights",
    )(*parts)


def caption_kernel(p_ref, out_ref, other, at_x, at_y, at_z, send, recv):
    me = coords()
    enter(me)
    copies = Copies(send, recv)
    copy = copies.start(p_ref, other, shifted(me, "core", 1))
    copy.wait_recv()
    other[...] = other[...] + p_ref[...]

    def exchange(axis, source, slots):
        waits = []
        for step in (2, 1, 3):
            peer = shifted(me, axis, step)
            waits.append(copies.start(source.at[peer[axis]], slots.at[me[axis]], peer))
        slots[me[axis]] = source[me[axis]]
        for copy in waits:
            copy.wait_recv()
        return (slots[0] + slots[1]) + (slots[2] + slots[3])

    sum_x = exchange("x", other, at_x)
    at_x2 = at_x.at[4]
    at_x2[...] = sum_x
    sum_y = exchange("y", at_x2, at_y)
    at_y2 = at_y.at[4]
    at_y2[...] = sum_y
    sum_z = exchange("z", at_y2, at_z)
    own = out_ref.at[me["x"], me["y"], me["z"]]
    own[...] = sum_z

    def spread(axis, view):
        waits = []
        for step in (2, 1, 3):
            waits.append(copies.start(view, view, shifted(me, axis, step)))
        for copy in waits:
            copy.wait_recv()

    spread("z", own)
    spread("y", out_ref.at[me["x"], me["y"]])
    spread("x", out_ref.at[me["x"]])
    copies.finish()


def sum_captions(partial):
    shape = (4, 4, 4, 8, 128)
    tiles = partial.reshape(16, 8, 4, 128).transpose(0, 2, 1, 3).reshape(shape)
    out = pl.pallas_call(
        caption_kernel,
        out_shape=jax.ShapeDtypeStruct(shape, jnp.float32),
        in_specs=[VM],
        out_specs=VM,
        scratch_shapes=[
            pltpu.VMEM(shape, jnp.float32),
            pltpu.VMEM((5, 4, 4, 8, 128), jnp.float32),
            pltpu.VMEM((5, 4, 8, 128), jnp.float32),
            pltpu.VMEM((4, 8, 128), jnp.float32),
            pltpu.SemaphoreType.DMA((19,)),
            pltpu.SemaphoreType.DMA((19,)),
        ],
        compiler_params=pltpu.CompilerParams(collective_id=2, has_side_effects=True),
        name="sum_captions",
    )(tiles)
    return out.reshape(16, 4, 8, 128).transpose(0, 2, 1, 3).reshape(128, 512)


def image_kernel(p_ref, out_ref, send, recv):
    me = coords()
    enter(me)
    copies = Copies(send, recv)
    pick(out_ref, me)[...] = p_ref[...]
    held = dict(me)
    first = True
    for axis in ("core", "z", "y", "x"):
        waits = []
        view = pick(out_ref, held)
        for step in (1,) if axis == "core" else (2, 1, 3):
            waits.append(copies.start(p_ref if first else view, view, shifted(me, axis, step)))
        first = False
        for copy in waits:
            copy.wait_recv()
        held.pop(axis)
    copies.finish()


def gather_images(pooled):
    tile = jnp.pad(pooled.reshape(6, 128), ((0, 10), (0, 0)))
    shape = (2, 4, 2, 4, 2, 16, 128)
    out = pl.pallas_call(
        image_kernel,
        out_shape=jax.ShapeDtypeStruct(shape, pooled.dtype),
        in_specs=[VM],
        out_specs=VM,
        scratch_shapes=[
            pltpu.SemaphoreType.DMA((10,)),
            pltpu.SemaphoreType.DMA((10,)),
        ],
        compiler_params=pltpu.CompilerParams(collective_id=3, has_side_effects=True),
        name="gather_images",
    )(tile)
    return out.reshape(128, 16, 128)[:, :6].reshape(128, 768)


ORDERS = (("x", "y", "z"), ("y", "z", "x"), ("z", "x", "y"))


def dims_of(axes):
    dims = []
    if "x" in axes:
        dims.append(2)
    if "y" in axes:
        dims.append(4)
    if "x" in axes:
        dims.append(2)
    if "z" in axes:
        dims.append(4)
    return tuple(dims)


def rest_of(order, phase):
    return [a for a in ("x", "y", "z") if a not in order[: phase + 1]]


def half_shape(order, phase):
    shape = dims_of(rest_of(order, phase)) + (BLK, 768)
    if len(shape) == 2:
        return (BLK, 384)
    return (shape[0] // 2,) + shape[1:]


def split(ref, side):
    if len(ref.shape) == 2:
        return ref.at[:, pl.ds(side * 384, 384)]
    return half(ref, side)


def add_into(dst, srcs, out=None):
    lead = dst.shape[:-2]
    total = 1
    for size in lead:
        total *= size

    def one(index):
        value = dst[index].astype(jnp.float32)
        for src in srcs:
            value = value + src[index].astype(jnp.float32)
        dst[index] = value.astype(dst.dtype)

    if total == 1:
        one((0,) * len(lead) + (slice(None), slice(None)))
        return

    def body(n, carry):
        index = []
        rest = n
        for size in reversed(lead):
            index.append(rest % size)
            rest = rest // size
        one(tuple(reversed(index)))
        return carry

    lax.fori_loop(0, total, body, 0)


def scatter_kernel(*refs):
    grads, s_ref = refs[0:3], refs[3]
    outs, s_out = refs[4:7], refs[7]
    accs = refs[8:11]
    hold = refs[11:29]
    s_slots, send, recv = refs[29], refs[30], refs[31]
    first = lambda t, p: hold[(t * 3 + p) * 2]
    second = lambda t, p: hold[(t * 3 + p) * 2 + 1]
    me = coords()
    enter(me)
    copies = Copies(send, recv)
    sibling = shifted(me, "core", 1)
    opening = []
    for t in range(3):
        opening.append(copies.start(grads[t].at[:, :, :, :, sibling["core"]], accs[t], sibling))
    s_wait = [copies.start(s_ref, s_slots.at[0, me["core"]], sibling)]
    s_slots[0, me["core"]] = s_ref[...]
    pending = [None] * 3
    held = [dict() for _ in range(3)]

    def open_phase(t, phase):
        axis = ORDERS[t][phase]
        far = shifted(me, axis, 2)
        view = pick(accs[t], {**held[t], axis: far[axis]})
        up, down = shifted(me, axis, 1), shifted(me, axis, 3)
        return (
            copies.start(split(view, 0), first(t, phase).at[0], up),
            copies.start(split(view, 1), first(t, phase).at[1], down),
        )

    for t in range(3):
        opening[t].wait_recv()
        add_into(accs[t], [grads[t].at[:, :, :, :, me["core"]]])
        pending[t] = open_phase(t, 0)
    for copy in s_wait:
        copy.wait_recv()
    s_value = s_slots[0, 0] + s_slots[0, 1]
    for phase in range(3):
        s_axis = ("x", "y", "z")[phase]
        s_slots[phase + 1, me[s_axis]] = s_value
        s_wait = []
        for step in (1, 2, 3):
            s_mine = s_slots.at[phase + 1, me[s_axis]]
            s_wait.append(copies.start(s_mine, s_mine, shifted(me, s_axis, step)))
        for t in range(3):
            axis = ORDERS[t][phase]
            up, down = shifted(me, axis, 1), shifted(me, axis, 3)
            to_up = pick(accs[t], {**held[t], axis: up[axis]})
            to_down = pick(accs[t], {**held[t], axis: down[axis]})
            pending[t][0].wait_recv()
            add_into(split(to_up, 0), [first(t, phase).at[0]])
            a = copies.start(to_up, second(t, phase).at[0], up)
            pending[t][1].wait_recv()
            add_into(split(to_down, 1), [first(t, phase).at[1]])
            b = copies.start(to_down, second(t, phase).at[1], down)
            pending[t] = (a, b)
        for t in range(3):
            axis = ORDERS[t][phase]
            pending[t][0].wait_recv()
            pending[t][1].wait_recv()
            held[t][axis] = me[axis]
            mine = pick(accs[t], held[t])
            if phase < 2:
                add_into(mine, [second(t, phase).at[0], second(t, phase).at[1]])
                pending[t] = open_phase(t, phase + 1)
            else:
                value = mine[...].astype(jnp.float32) + second(t, phase)[0].astype(jnp.float32)
                value = value + second(t, phase)[1].astype(jnp.float32)
                outs[t][...] = value[: outs[t].shape[0]]
        for copy in s_wait:
            copy.wait_recv()
        s_value = (s_slots[phase + 1, 0] + s_slots[phase + 1, 1]) + (
            s_slots[phase + 1, 2] + s_slots[phase + 1, 3]
        )
    s_out[...] = s_value
    copies.finish()


def scatter_grads(grads, rows, scalar):
    lead = (2, 4, 2, 4, 2, BLK, 768)
    grads = [g.reshape(lead) for g in grads]
    tile = jnp.full((8, 128), scalar, jnp.float32)
    scratch = [pltpu.VMEM((2, 4, 2, 4, BLK, 768), jnp.bfloat16) for _ in range(3)]
    for t in range(3):
        for phase in range(3):
            scratch.append(pltpu.VMEM((2,) + half_shape(ORDERS[t], phase), jnp.bfloat16))
            scratch.append(
                pltpu.VMEM((2,) + dims_of(rest_of(ORDERS[t], phase)) + (BLK, 768), jnp.bfloat16)
            )
    scratch += [
        pltpu.VMEM((4, 4, 8, 128), jnp.float32),
        pltpu.SemaphoreType.DMA((49,)),
        pltpu.SemaphoreType.DMA((49,)),
    ]
    return pl.pallas_call(
        scatter_kernel,
        out_shape=[jax.ShapeDtypeStruct((r, 768), jnp.float32) for r in rows]
        + [jax.ShapeDtypeStruct((8, 128), jnp.float32)],
        in_specs=[VM] * 4,
        out_specs=[VM] * 4,
        scratch_shapes=scratch,
        compiler_params=pltpu.CompilerParams(
            collective_id=4, has_side_effects=True, vmem_limit_bytes=48 * 1024 * 1024
        ),
        name="scatter_grads",
    )(*grads, tile)


def gelu_tanh(values):
    return jax.nn.gelu(values, approximate=True)


def pad_blocks(values, size, axis):
    shape = values.shape
    blocks = shape[axis] // size
    cut = values.reshape(shape[:axis] + (blocks, size) + shape[axis + 1 :])
    pads = [(0, 0)] * cut.ndim
    pads[axis + 1] = (0, BLK - size)
    return jnp.pad(cut, pads).reshape(shape[:axis] + (blocks * BLK,) + shape[axis + 1 :])


def unit_rows(values):
    return values / jnp.sqrt(jnp.sum(values * values, -1, keepdims=True) + 1e-06)


def dot(a, b, da, db):
    return lax.dot_general(a, b, (((da,), (db,)), ((), ())), preferred_element_type=jnp.float32)


def local(
    teacher_in,
    teacher_gain,
    teacher_up,
    teacher_down,
    student_in,
    student_gain,
    student_up,
    student_down,
    student_head,
    student_proj,
    word_table,
    caption_ids,
    positive,
):
    grp_index = lax.axis_index("grp")
    dp_index = lax.axis_index("dp")
    n_grp = lax.axis_size("grp")
    n_dp = lax.axis_size("dp")
    shard = grp_index * n_dp + dp_index
    width = teacher_in.shape[1]
    feat = width // (n_grp * n_dp)
    hid = student_up.shape[1]
    own_rows = teacher_in.shape[0] // n_grp

    proj_cols = student_proj.shape[1]
    parts = [
        pad_blocks(teacher_up, feat, 0),
        pad_blocks(teacher_down, feat, 0),
        pad_blocks(student_up.T, hid, 0),
        pad_blocks(student_down, hid, 0),
        pad_blocks(student_head.T, feat, 0),
        jnp.pad(student_proj.T, ((0, BLK - proj_cols), (0, 0))),
    ]
    t_up, t_down, s_up, s_down, s_head, s_proj = gather_weights(parts)
    t_up = t_up.reshape(-1, t_up.shape[-1])
    t_down = t_down.reshape(-1, t_down.shape[-1])
    s_up, s_down, s_head = (v.reshape(-1, v.shape[-1]) for v in (s_up, s_down, s_head))
    s_proj = s_proj.reshape(-1, BLK, s_proj.shape[-1])[:, :proj_cols]
    s_proj = s_proj.reshape(-1, s_proj.shape[-1])

    vocab_dev = word_table.shape[0]
    vocab_codes = shard * vocab_dev + jnp.arange(vocab_dev, dtype=jnp.int32)
    counts = jnp.sum(
        caption_ids[:, :, None] == vocab_codes[None, None, :], 1, dtype=jnp.float32
    ).astype(jnp.bfloat16)
    partial_words = jnp.dot(counts, word_table, preferred_element_type=jnp.float32) / CAP_LEN
    caption_all = unit_rows(sum_captions(partial_words))

    wide = t_up.shape[0]
    place = jnp.arange(width, dtype=jnp.int32)
    place = place // feat * BLK + place % feat
    spread_map = (place[:, None] == jnp.arange(wide, dtype=jnp.int32)[None, :]).astype(jnp.bfloat16)
    teacher_wide = dot(teacher_in, spread_map, 1, 0).astype(jnp.bfloat16)
    gain_wide = pad_blocks(teacher_gain, feat, 0)
    real = (jnp.arange(wide, dtype=jnp.int32) % BLK < feat)[None, :]
    values = teacher_wide.astype(jnp.float32)
    mean = jnp.sum(values, -1, keepdims=True) / width
    center = jnp.where(real, values - mean, 0.0)
    variance = jnp.sum(center * center, -1, keepdims=True) / width
    teacher_normed = (center * lax.rsqrt(variance + 1e-05) * gain_wide).astype(jnp.bfloat16)
    teacher_act = gelu_tanh(dot(teacher_normed, t_up, 1, 0)).astype(jnp.bfloat16)
    branch = dot(teacher_act, t_down, 1, 1).astype(jnp.bfloat16)
    branch_own = lax.dynamic_slice_in_dim(branch, grp_index * own_rows, own_rows, 0)
    branch_far = lax.dynamic_slice_in_dim(branch, (1 - grp_index) * own_rows, own_rows, 0)
    branch_got = lax.ppermute(branch_far, "grp", [(0, 1), (1, 0)])
    teacher_own = lax.dynamic_slice_in_dim(teacher_wide, grp_index * own_rows, own_rows, 0)

    rows = lax.dynamic_slice_in_dim(student_in, grp_index * own_rows, own_rows, 0).astype(
        jnp.float32
    )
    center = rows - jnp.mean(rows, -1, keepdims=True)
    variance = jnp.mean(center * center, -1, keepdims=True)
    normed = (center * lax.rsqrt(variance + 1e-05) * student_gain).astype(jnp.bfloat16)
    gate_out = dot(normed, s_up, 1, 1)
    act = gelu_tanh(gate_out).astype(jnp.bfloat16)
    student_out = rows + dot(act, s_down, 1, 0)
    rounded = student_out.astype(jnp.bfloat16)
    pooled = (jnp.sum(student_out, 0, keepdims=True) / PATCHES).astype(jnp.bfloat16)

    pooled_all = gather_images(pooled)
    projected = dot(pooled_all, s_proj, 1, 1)
    proj_norm = jnp.sqrt(jnp.sum(projected * projected, -1, keepdims=True) + 1e-06)
    image_emb = projected / proj_norm
    scores = 100.0 * jnp.dot(image_emb, caption_all.T, precision=lax.Precision.HIGHEST)
    target_of = positive.reshape(n_dp, n_grp).T.reshape(-1)
    match = (target_of[:, None] == jnp.arange(scores.shape[1], dtype=jnp.int32)[None, :]).astype(
        jnp.float32
    )
    contrast = (
        jnp.sum(jax.nn.logsumexp(scores, 1))
        + jnp.sum(jax.nn.logsumexp(scores, 0))
        - 2.0 * jnp.sum(match * scores)
    )
    grad_scores = jax.nn.softmax(scores, 1) + jax.nn.softmax(scores, 0) - 2.0 * match
    grad_image = 100.0 * jnp.dot(grad_scores, caption_all, precision=lax.Precision.HIGHEST)
    grad_projected = (
        (grad_image - image_emb * jnp.sum(image_emb * grad_image, -1, keepdims=True)) / proj_norm
    ).astype(jnp.bfloat16)
    grad_columns = lax.dynamic_slice_in_dim(grad_projected, shard * proj_cols, proj_cols, 1)
    grad_proj = dot(grad_columns, pooled_all, 0, 0).T
    grad_projected_own = lax.dynamic_slice_in_dim(grad_projected, shard, 1, 0)
    grad_pooled = dot(grad_projected_own, s_proj, 1, 0)

    target = teacher_own.astype(jnp.float32) + (
        branch_own.astype(jnp.float32) + branch_got.astype(jnp.float32)
    )
    diff = dot(rounded, s_head, 1, 1) - target
    feature_part = jnp.sum(diff * diff) / width
    grad_pred = (2.0 * diff / width).astype(jnp.bfloat16)
    head_part = dot(grad_pred, rounded, 0, 0).astype(jnp.bfloat16)
    grad_out = (dot(grad_pred, s_head, 1, 0) + grad_pooled / PATCHES).astype(jnp.bfloat16)
    down_part = dot(act, grad_out, 0, 0).astype(jnp.bfloat16)
    grad_act = dot(grad_out, s_down, 1, 1)
    grad_gate = jax.vjp(gelu_tanh, gate_out)[1](grad_act)[0].astype(jnp.bfloat16)
    up_part = dot(grad_gate, normed, 0, 0).astype(jnp.bfloat16)
    grad_up, grad_down, grad_head, feature = scatter_grads(
        (up_part, down_part, head_part), (hid, hid, feat), feature_part
    )
    loss = (feature[0, 0] + contrast) / (positive.shape[0] * PATCHES)
    return (loss, grad_up.T, grad_down, grad_head.T, grad_proj)


def solution(mesh):
    placed = (
        P("dp", None),
        P(),
        P("dp", "grp"),
        P("dp", "grp"),
        P("dp", None),
        P(),
        P(None, ("grp", "dp")),
        P(("grp", "dp"), None),
        P(None, ("grp", "dp")),
        P(None, ("grp", "dp")),
        P(("grp", "dp"), None),
        P(),
        P(),
    )
    return jax.shard_map(
        local,
        mesh=mesh,
        in_specs=placed,
        out_specs=(
            P(),
            P(None, ("grp", "dp")),
            P(("grp", "dp"), None),
            P(None, ("grp", "dp")),
            P(None, ("grp", "dp")),
        ),
        check_vma=False,
    )
```

time: 1870 us -> 274 us (0.15)
  blocking collectives: 788 us -> 0 us
  waiting for transfers between devices: 669 us -> 0.01 us
  starting transfers between devices: 234 us -> 0.27 us
  Pallas kernels: 0 us -> 190 us
  local copies, waits for them, and re-layouts: 80.9 us -> 19.5 us
  between operations: 24.5 us -> 5.39 us
    all_gather x5 -> x0, waiting for transfers between devices: 541 us -> none  [the longest x1 192 us: local(): lax.all_gather(student_up, ('grp', 'dp'), axis=1, tiled=True)]
    unnamed x1 -> x0, blocking collectives: 367 us -> none
    all_gather x2 -> x0, blocking collectives: 357 us -> none  [the longest x1 181 us: local(): lax.all_gather(student_proj, ('grp', 'dp'), axis=1, tiled=True)]
    unnamed x90 -> x0, starting transfers between devices: 233 us -> none
    pallas_call x0 -> x4, Pallas kernels: none -> 190 us  [the longest x1 91.4 us: gather_weights(): pl.pallas_call(weight_kernel, out_shape=outs, in_specs=[ANY] * 6, out_spe...]
    unnamed x99 -> x0, waiting for transfers between devices: 103 us -> none
    unnamed x127 -> x40, local copies, waits for them, and re-layouts: 75.8 us -> 5.94 us
    psum x1 -> x0, blocking collectives: 63.5 us -> none  [local(): total = lax.psum(feature_part + contrast_part, ('grp', 'dp'))]
  transfers between devices with their start and end apart: 97 -> 1, of which waited for: 6 -> 0; matrix products, arithmetic and copies ran while one was open for 27% -> 8% of each run, Pallas kernels for 0% -> 20%
where the time goes in v1:
time: 274 us; the launch traced here: 273 us
  Pallas kernels  190 us (69%)
  matrix products  51.9 us (19%)
  local copies, waits for them, and re-layouts  19.5 us (7%)
  other arithmetic  6.07 us (2%)
  between operations  5.39 us (2%)
    pallas_call x1, Pallas kernels, gather_weights(): pl.pallas_call(weight_kernel, out_shape=outs, in_specs=[ANY] * 6, out_spe...  91.4 us
    dot_general x12, matrix products, dot(): lax.dot_general(a, b, (((da,), (db,)), ((), ())), preferred_element_type=...  46.8 us
    pallas_call x1, Pallas kernels, scatter_grads(): pl.pallas_call(scatter_kernel, out_shape=[jax.ShapeDtypeStruct((r, 768),...  44.6 us
    pallas_call x1, Pallas kernels, sum_captions(): pl.pallas_call(caption_kernel, out_shape=jax.ShapeDtypeStruct(shape, jnp....  27.9 us
    pallas_call x1, Pallas kernels, gather_images(): pl.pallas_call(image_kernel, out_shape=jax.ShapeDtypeStruct(shape, pooled...  25.9 us
    unnamed x40, local copies, waits for them, and re-layouts  5.94 us
  transfers between devices with their start and end apart: 1, of which 0 were waited for; matrix products, arithmetic and copies ran while one was open for 8% of the time, Pallas kernels for 20%

profile of v1, /device:TPU:0, one launch (start us, length us, event | category | flops | bytes accessed | tf_op | source)
XLA Modules:
  0.0 273.0 jit_solution(12020691293037016384)
XLA Ops:
  0.7 1.1 reshape.201
  1.7 0.9 reshape.203
  2.7 0.7 pad.30
  3.3 0.7 pad.31
  4.0 1.3 pad.35.refs_5_
  5.3 1.4 pad_bitcast_fusion.2.refs_2_
  6.7 4.9 %convert_reduce_fusion.1 = (f32[512]{0:T(512)S(1)}, bf16[2048,512]{0,1:T(8,128)(2,1)S(1)}) fusion(bf16[512,1664]{1,0:T(8,128)(2,1)S(1)} %copy-done, s32[1664]{0:T(1024)S(1)} %fusion.73), kind=kOutput, calls=%fused_computation.6 | convolution fusion | flops 3496214016 | bytes 3809792 | tf_op jit(solution)/shard_map/dot_general | solution.py:497
  11.7 1.3 copy-done.2
  13.0 0.8 fusion.5
  14.8 91.4 %gather_weights.1 = (bf16[4,2,4,2,32,2048]{5,4,3,2,1,0:T(8,128)(2,1)}, bf16[4,2,4,2,32,2048]{5,4,3,2,1,0:T(8,128)(2,1)}, bf16[2,4,2,4,2,16,768]{6,5,4,3,2,1,0:T(...) custom-call(bf16[32,2048]{1,0:T(8,128)(2,1)} %bitcast.87, ...), custom_call_target="tpu_custom_call" | custom-call | tf_op jit(solution)/shard_map/gather_weights/pallas_call | solution.py:195
  106.2 16.8 %convolution_convert_fusion.3 = bf16[512,2048]{1,0:T(8,128)(2,1)} fusion(bf16[2048,2048]{1,0:T(8,128)(2,1)} %bitcast.96, bf16[2048,2048]{1,0:T(8,128)(2,1)} %bitcast.95, bf16[2048,512]{0,1:T(8,128)(2,1)} %copy-done.2, f32[2048]{0:T(1024)S(1)} %mul.197, f32[512]{0:T(512)S(1)} %add_rsqrt_fusion, f32[512]{0:T(512)S(1)} %broadcast_multiply_fusion.1, ...), kind=kOutput, calls=%fused_computation.27 | convolution fusion | flops 8606711808 | bytes 20985856 | tf_op jit(solution)/shard_map/dot_general | solution.py:497
  123.0 2.4 constant_dynamic-slice_fusion
  126.1 3.1 %fusion.100 = f32[256,2048]{1,0:T(8,128)S(1)} fusion(bf16[2048,768]{1,0:T(8,128)(2,1)} %bitcast.78, f32[768]{0:T(1024)S(1)} %copy-done.14, f32[256]{0:T(256)S(1)} %add_rsqrt_fusion.1, f32[256]{0:T(256)S(1)} %broadcast_multiply_fusion.2, bf16[512,768]{1,0:T(8,128)(2,1)S(1)} %copy-done.8, s32[]{:T(128)S(6)} %select_n.65), kind=kOutput, calls=%fused_computation.152 | convolution fusion | flops 806289408 | bytes 5642244 | tf_op jit(solution)/shard_map/dot_general | solution.py:497
  129.3 2.1 fusion.103
  132.0 25.9 %gather_images.1 = bf16[2,4,2,4,2,16,128]{6,5,4,3,2,1,0:T(8,128)(2,1)} custom-call(bf16[16,128]{1,0:T(8,128)(2,1)} %pad.37.p_ref), custom_call_target="tpu_custom_call" | custom-call | tf_op jit(solution)/shard_map/gather_images/pallas_call | solution.py:295
  157.9 1.0 slice.12
  159.1 1.6 slice.13
  161.4 1.6 convert_reduce_fusion
  163.1 2.0 convolution_multiply_fusion.1
  165.0 27.9 %sum_captions.1 = f32[4,4,4,8,128]{4,3,2,1,0:T(8,128)} custom-call(f32[4,4,4,8,128]{4,3,2,1,0:T(8,128)} %bitcast.83), custom_call_target="tpu_custom_call" | custom-call | tf_op jit(solution)/shard_map/sum_captions/pallas_call | solution.py:254
  193.0 1.0 multiply_reduce_fusion.2
  194.1 1.5 fusion.102
  196.0 0.8 select_reduce_fusion
  199.9 1.7 multiply_reduce_fusion.1
  202.0 0.9 fusion.57
  202.9 4.0 %multiply_reduce_fusion = (f32[]{:T(128)}, f32[256,2048]{1,0:T(8,128)S(1)}) fusion(bf16[256,2048]{1,0:T(8,128)(2,1)} %collective-permute-done, bf16[512,2048]{1,0:T(8,128)(2,1)S(1)} %copy-done.5, s32[]{:T(128)S(6)} %select_n.65, bf16[2048,512]{0,1:T(8,128)(2,1)S(1)} %copy-done.3, bf16[2048,768]{1,0:T(8,128)(2,1)} %bitcast.76, ...), kind=kOutput, calls=%fused_computation.40 | convolution fusion | flops 809500672 | bytes 8781832 | tf_op jit(solution)/shard_map/dot_general | solution.py:497
  206.9 2.7 convolution_convert_fusion
  209.6 1.0 fusion.37
  211.2 3.3 %convolution_convert_fusion.1 = bf16[2048,768]{1,0:T(8,128)(2,1)} fusion(bf16[256,768]{1,0:T(8,128)(2,1)S(1)} %fusion.37, f32[256,2048]{1,0:T(8,128)S(1)} %copy-done.7), kind=kOutput, calls=%fused_computation.22 | convolution fusion | flops 811597824 | bytes 5636096 | tf_op jit(solution)/shard_map/dot_general | solution.py:497
  214.4 7.3 %convolution_convert_fusion.2 = bf16[2048,768]{1,0:T(8,128)(2,1)} fusion(f32[256,2048]{1,0:T(8,128)} %copy-done.6, f32[768]{0:T(1024)S(1)} %copy-done.14, f32[256]{0:T(256)S(1)} %add_rsqrt_fusion.1, f32[256]{0:T(256)S(1)} %broadcast_multiply_fusion.2, bf16[512,768]{1,0:T(8,128)(2,1)S(1)} %copy-done.9, s32[]{:T(128)S(6)} %select_n.65, ...), kind=kOutput, calls=%fused_computation.23 | convolution fusion | flops 1623654400 | bytes 9181188 | tf_op jit(solution)/shard_map/dot_general | solution.py:497
  222.4 1.9 copy-done.1
  224.3 44.6 %scatter_grads.1 = (f32[12,768]{1,0:T(8,128)S(1)}, f32[12,768]{1,0:T(8,128)S(1)}, f32[13,768]{1,0:T(8,128)S(1)}, f32[8,128]{1,0:T(8,128)S(1)}) custom-call(bf16[2,4,2,4,2,16,768]{6,5,4,3,2,1,0:T(8,128)(2,1)S(1)} %bitcast.72, bf16[2,4,2,4,2,16,768]{6,5,4,3,2,1,0:T(8,128)(2,1)} %bitcast.79, bf16[2,4,2,4,2,16,768]{6,5,4,3,2,1,0:T(8,128)(2,1)} %bitcast.75, ...), custom_call_target="tpu_custom_call" | custom-call | tf_op jit(solution)/shard_map/scatter_grads/pallas_call | solution.py:465
  (72 shorter events, 8.1 us)
Async XLA Ops:
  0.6 6.0 %copy-start = (bf16[512,1664]{1,0:T(8,128)(2,1)S(1)}, bf16[512,1664]{1,0:T(8,128)(2,1)}, u32[]{:S(2)}) copy-start(bf16[512,1664]{1,0:T(8,128)(2,1)} %param.13) | copy-start | bytes 5111812
  11.6 1.4 copy-start.2
  11.6 2.2 copy-start.15
  11.6 2.5 copy-start.12
  11.6 2.5 copy-start.13
  123.0 2.7 copy-start.8
  123.0 3.1 %copy-start.14 = (f32[768]{0:T(1024)S(1)}, f32[768]{0:T(1024)}, u32[]{:S(2)}) copy-start(f32[768]{0:T(1024)} %param.18) | copy-start | bytes 9220
  125.4 77.4 %collective-permute-start = (bf16[256,2048]{1,0:T(8,128)(2,1)}, bf16[256,2048]{1,0:T(8,128)(2,1)}, u32[]{:S(2)}, u32[]{:S(2)}) collective-permute-start(bf16[256,2048]{1,0:T(8,128)(2,1)} %constant_dynamic-slice_fusion), channel_id=1, source_target_pairs={{0,64},{64,0},{1,65},{65,1},{2,66},{66,2},{3,67},{67,3},{4,68},{68... | collective-permute-start | bytes 3145736 | tf_op jit(solution)/shard_map/ppermute | solution.py:565
  126.1 3.1 %copy-start.17 = (bf16[2,4,2,4,2,16,768]{6,5,4,3,2,1,0:T(8,128)(2,1)S(1)}, bf16[2,4,2,4,2,16,768]{6,5,4,3,2,1,0:T(8,128)(2,1)}, u32[]{:S(2)}) copy-start(bf16[2,4,2,4,2,16,768]{6,5,4,3,2,1,0:T(8,128)(2,1)} %get-tuple-element.16) | copy-start | bytes 9437188
  129.2 2.1 copy-start.6
  159.1 2.3 copy-start.11
  161.4 34.3 %copy-start.16 = (s32[128]{0:T(128)S(1)}, s32[128]{0:T(128)}, u32[]{:S(2)}) copy-start(s32[128]{0:T(128)} %param.25) | copy-start | bytes 1540
  194.1 8.8 %copy-start.10 = (bf16[256,768]{1,0:T(8,128)(2,1)S(1)}, bf16[256,768]{1,0:T(8,128)(2,1)}, u32[]{:S(2)}) copy-start(bf16[256,768]{1,0:T(8,128)(2,1)} %get-tuple-element.35) | copy-start | bytes 1179652
  199.9 3.0 %copy-start.3 = (bf16[2048,512]{0,1:T(8,128)(2,1)S(1)}, bf16[2048,512]{0,1:T(8,128)(2,1)}, u32[]{:S(2)}) copy-start(bf16[2048,512]{0,1:T(8,128)(2,1)} %copy-done.2) | copy-start | bytes 6291460
  199.9 3.0 %copy-start.5 = (bf16[512,2048]{1,0:T(8,128)(2,1)S(1)}, bf16[512,2048]{1,0:T(8,128)(2,1)}, u32[]{:S(2)}) copy-start(bf16[512,2048]{1,0:T(8,128)(2,1)} %convolution_convert_fusion.3) | copy-start | bytes 6291460
  206.9 2.7 copy-start.4
  209.6 1.6 copy-start.7
  211.2 3.3 %copy-start.9 = (bf16[512,768]{1,0:T(8,128)(2,1)S(1)}, bf16[512,768]{1,0:T(8,128)(2,1)}, u32[]{:S(2)}) copy-start(bf16[512,768]{1,0:T(8,128)(2,1)} %param.17) | copy-start | bytes 2359300
  222.4 1.9 copy-start.1
